TPU v7x, 32 devices: a whole 2x2x4 slice. The times are simulated.
32 devices in a mesh: band: 4 (over y, x), grid: 8 (over z, core).
Axes of the slice: x: 2, y: 2, z: 4, core: 2. Of those that a mesh axis runs over, the one named last changes fastest.
Arguments:
- wavefunctions: bfloat16 [1024, 131072], P('band', 'grid'), may hold values from -6 to 6
- projectors: bfloat16 [512, 8, 13, 256], P('grid'), may hold values from -0.0068359375 to 0.0068359375
- slot_atom: int32 [512, 8], P('grid'), may hold values from -1 to 255, as said below
- occupations: float32 [1024], P('band'), may hold values from 0.02 to 2
Outputs:
- density: float32 [256, 13, 13], P('grid')
Inputs may be any that keep to these rules, and one draw needn't show every extreme that they name: `slot_atom`: -1 marks an empty slot. Any other entry is an atom a whose owning domain a // 32 lies within 3 domains, counted around the closed cycle of 8 domains, of the domain of the block, block index // 64. In every domain some block has all 8 slots filled.
All inputs are finite; a program needn't handle non-finite values.
Results may differ from a plain program's by a relative error of at most 0.0003.
Values sent between devices are 32-bit elements; how exact they have to be, the bound alone decides.
A program may use at most 64 MiB of HBM per device.

v0:
```python
import jax
import jax.numpy as jnp
from jax import lax
from jax.sharding import PartitionSpec as P

REACH = 3
ATOMS_DEV = 32


def shifted(block, axis, distance):
    devices = range(lax.axis_size(axis))
    route = [((i - distance) % len(devices), i) for i in devices]
    return lax.ppermute(block, axis, route)


def body(wavefunctions, projectors, slot_atom, occupations):
    band_count = wavefunctions.shape[0]
    block_count, capacity, proj_count, block_len = projectors.shape
    domains = lax.axis_size("grid")
    domain = lax.axis_index("grid")
    window_len = 2 * REACH + 1
    row_len = proj_count * band_count
    grid_blocks = wavefunctions.reshape(band_count, block_count, block_len)
    stacked = projectors.reshape(block_count, capacity * proj_count, block_len)
    slot_terms = jnp.einsum(
        "ngb,gcb->gcn", grid_blocks, stacked, preferred_element_type=jnp.float32
    )
    slot_terms = slot_terms.reshape(block_count * capacity, row_len)
    slot_ids = slot_atom.reshape(-1)
    owner = jnp.floor_divide(slot_ids, ATOMS_DEV)
    offset = jnp.mod(owner - domain + REACH, domains)
    target = jnp.where(
        slot_ids >= 0, offset * ATOMS_DEV + jnp.mod(slot_ids, ATOMS_DEV), window_len * ATOMS_DEV
    )
    selector = (
        jnp.arange(window_len * ATOMS_DEV, dtype=jnp.int32)[:, None] == target[None, :]
    ).astype(jnp.float32)
    window = jnp.dot(
        selector, slot_terms, precision=lax.Precision.HIGHEST, preferred_element_type=jnp.float32
    )
    window = window.reshape(window_len, ATOMS_DEV, row_len)
    forward = window[2 * REACH]
    for hop in range(REACH, 0, -1):
        forward = shifted(forward, "grid", 1) + window[REACH + hop - 1]
    backward = window[0]
    for hop in range(REACH, 0, -1):
        addend = window[REACH - hop + 1] if hop > 1 else jnp.zeros_like(backward)
        backward = shifted(backward, "grid", -1) + addend
    owned = forward + backward
    owned = owned.reshape(ATOMS_DEV, proj_count, band_count)
    weighted = owned * occupations.reshape(1, 1, band_count)
    partial_sum = jnp.einsum("ain,ajn->aij", weighted, owned, precision=lax.Precision.HIGHEST)
    density = lax.psum(partial_sum, "band")
    return density


def solution(mesh):
    in_specs = (P("band", "grid"), P("grid", None, None, None), P("grid", None), P("band"))
    out_specs = P("grid", None, None)
    return jax.shard_map(body, mesh=mesh, in_specs=in_specs, out_specs=out_specs, check_vma=False)
```

profile of v0, /device:TPU:0, one launch (start us, length us, event | category | flops | bytes accessed | tf_op | source)
XLA Modules:
  0.0 87.4 jit_solution(6354588679132287062)
XLA Ops:
  0.0 2.8 %copy.8 = bf16[64,8,13,256]{3,0,2,1:T(8,128)(2,1)S(1)} copy(bf16[64,8,13,256]{3,1,2,0:T(8,128)(2,1)} %param.5) | data formatting | bytes 6815744 | tf_op args[1]
  2.8 9.4 %fusion = f32[64,104,256]{2,1,0:T(8,128)} fusion(bf16[32,64,8,256]{3,2,1,0:T(8,128)(2,1)} %bitcast.8, bf16[64,104,256]{2,0,1:T(8,128)(2,1)S(1)} %bitcast.7), kind=kOutput, calls=%fused_computation | convolution fusion | flops 872415232 | bytes 18612224 | tf_op jit(solution)/shard_map/ngb,gcb->gcn/dot_general | solution.py:25
  12.2 8.5 %reshape.103 = f32[512,3328]{1,0:T(8,128)} reshape(f32[64,104,256]{2,1,0:T(8,128)} %fusion) | data formatting | bytes 13631488 | tf_op jit(solution)/shard_map/reshape | solution.py:28
  20.7 0.1 copy.7
  20.7 0.1 reshape.100
  20.9 6.3 %fusion.6 = f32[224,3328]{1,0:T(8,128)S(1)} fusion(f32[512,3328]{1,0:T(8,128)} %reshape.103, s32[512]{0:T(512)S(1)} %fusion.15), kind=kOutput, calls=%fused_computation.7 | convolution fusion | flops 4580294656 | bytes 9799680 | tf_op jit(solution)/shard_map/dot_general | solution.py:38
  27.2 0.5 collective-permute-start
  27.8 4.1 %collective-permute-start.3 = (f32[32,3328]{1,0:T(8,128)S(1)}, f32[32,3328]{1,0:T(8,128)S(1)}, u32[]{:S(2)}, u32[]{:S(2)}) collective-permute-start(f32[32,3328]{1,0:T(8,128)S(1)} %get-tuple-element.10), channel_id=1, source_target_pairs={{1,0},{2,1},{3,2},{4,3},{5,4},{6,5},{7,6},{0,7},{9,8},{10,9},{11,1... | collective-permute-start | bytes 1277960 | tf_op jit(solution)/shard_map/ppermute | solution.py:13
  31.9 7.7 %collective-permute-done = f32[32,3328]{1,0:T(8,128)S(1)} collective-permute-done((f32[32,3328]{1,0:T(8,128)S(1)}, f32[32,3328]{1,0:T(8,128)S(1)}, u32[]{:S(2)}, u32[]{:S(2)}) %collective-permute-start) | collective-permute-done | bytes 426016 | tf_op jit(solution)/shard_map/ppermute | solution.py:13
  39.6 0.4 collective-permute-done.3
  40.0 0.1 slice_add_fusion.4
  40.1 2.0 %collective-permute-start.1 = (f32[32,3328]{1,0:T(8,128)S(1)}, f32[32,3328]{1,0:T(8,128)S(1)}, u32[]{:S(2)}, u32[]{:S(2)}) collective-permute-start(f32[32,3328]{1,0:T(8,128)S(1)} %get-tuple-element.7), channel_id=1, source_target_pairs={{7,0},{0,1},{1,2},{2,3},{3,4},{4,5},{5,6},{6,7},{15,8},{8,9},{9,10... | collective-permute-start | bytes 1277960 | tf_op jit(solution)/shard_map/ppermute | solution.py:13
  42.1 1.8 %collective-permute-start.4 = (f32[32,3328]{1,0:T(8,128)S(1)}, f32[32,3328]{1,0:T(8,128)S(1)}, u32[]{:S(2)}, u32[]{:S(2)}) collective-permute-start(f32[32,3328]{1,0:T(8,128)S(1)} %get-tuple-element.8), channel_id=1, source_target_pairs={{1,0},{2,1},{3,2},{4,3},{5,4},{6,5},{7,6},{0,7},{9,8},{10,9},{11,1... | collective-permute-start | bytes 1277960 | tf_op jit(solution)/shard_map/ppermute | solution.py:13
  44.0 7.6 %collective-permute-done.1 = f32[32,3328]{1,0:T(8,128)S(1)} collective-permute-done((f32[32,3328]{1,0:T(8,128)S(1)}, f32[32,3328]{1,0:T(8,128)S(1)}, u32[]{:S(2)}, u32[]{:S(2)}) %collective-permute-start.1) | collective-permute-done | bytes 426016 | tf_op jit(solution)/shard_map/ppermute | solution.py:13
  51.5 0.2 collective-permute-done.4
  51.7 0.1 slice_add_fusion.3
  51.8 2.5 %collective-permute-start.2 = (f32[32,3328]{1,0:T(8,128)S(1)}, f32[32,3328]{1,0:T(8,128)S(1)}, u32[]{:S(2)}, u32[]{:S(2)}) collective-permute-start(f32[32,3328]{1,0:T(8,128)S(1)} %get-tuple-element.5), channel_id=1, source_target_pairs={{7,0},{0,1},{1,2},{2,3},{3,4},{4,5},{5,6},{6,7},{15,8},{8,9},{9,10... | collective-permute-start | bytes 1277960 | tf_op jit(solution)/shard_map/ppermute | solution.py:13
  54.2 1.4 %collective-permute-start.5 = (f32[32,3328]{1,0:T(8,128)S(1)}, f32[32,3328]{1,0:T(8,128)S(1)}, u32[]{:S(2)}, u32[]{:S(2)}) collective-permute-start(f32[32,3328]{1,0:T(8,128)S(1)} %get-tuple-element.6), channel_id=1, source_target_pairs={{1,0},{2,1},{3,2},{4,3},{5,4},{6,5},{7,6},{0,7},{9,8},{10,9},{11,1... | collective-permute-start | bytes 1277960 | tf_op jit(solution)/shard_map/ppermute | solution.py:13
  55.7 7.1 %collective-permute-done.2 = f32[32,3328]{1,0:T(8,128)S(1)} collective-permute-done((f32[32,3328]{1,0:T(8,128)S(1)}, f32[32,3328]{1,0:T(8,128)S(1)}, u32[]{:S(2)}, u32[]{:S(2)}) %collective-permute-start.2) | collective-permute-done | bytes 426016 | tf_op jit(solution)/shard_map/ppermute | solution.py:13
  62.8 1.0 %collective-permute-done.5 = f32[32,3328]{1,0:T(8,128)S(1)} collective-permute-done((f32[32,3328]{1,0:T(8,128)S(1)}, f32[32,3328]{1,0:T(8,128)S(1)}, u32[]{:S(2)}, u32[]{:S(2)}) %collective-permute-start.5) | collective-permute-done | bytes 426016 | tf_op jit(solution)/shard_map/ppermute | solution.py:13
  63.9 0.1 reshape.104
  64.0 0.6 fusion.4
  64.7 21.9 %psum.7 = f32[32,13,13]{2,1,0:T(8,128)S(1)} all-reduce(f32[32,13,13]{2,1,0:T(8,128)S(1)} %fusion.4), channel_id=1, replica_groups=mesh['band'=4,'grid'=8] {'band'}, use_global_device_ids=true, to_apply=%region_0.1 | all-reduce | flops 5408 | bytes 43264 | tf_op jit(solution)/shard_map/psum | solution.py:53
  86.6 0.8 copy.11
  (7 shorter events, 0.1 us)
Async XLA Ops:
  12.2 8.5 %copy-start = (s32[64,8]{0,1:T(8,128)S(1)}, s32[64,8]{0,1:T(8,128)}, u32[]{:S(2)}) copy-start(s32[64,8]{0,1:T(8,128)} %param.6) | copy-start | bytes 6148
  27.2 12.3 %collective-permute-start = (f32[32,3328]{1,0:T(8,128)S(1)}, f32[32,3328]{1,0:T(8,128)S(1)}, u32[]{:S(2)}, u32[]{:S(2)}) collective-permute-start(f32[32,3328]{1,0:T(8,128)S(1)} %get-tuple-element.9), channel_id=1, source_target_pairs={{7,0},{0,1},{1,2},{2,3},{3,4},{4,5},{5,6},{6,7},{15,8},{8,9},{9,10... | collective-permute-start | bytes 1277960 | tf_op jit(solution)/shard_map/ppermute | solution.py:13
  27.8 36.3 %copy-start.1 = (f32[256]{0:T(256)S(1)}, f32[256]{0:T(256)}, u32[]{:S(2)}) copy-start(f32[256]{0:T(256)} %param.7) | copy-start | bytes 3076
  27.8 12.2 %collective-permute-start.3 = (f32[32,3328]{1,0:T(8,128)S(1)}, f32[32,3328]{1,0:T(8,128)S(1)}, u32[]{:S(2)}, u32[]{:S(2)}) collective-permute-start(f32[32,3328]{1,0:T(8,128)S(1)} %get-tuple-element.10), channel_id=1, source_target_pairs={{1,0},{2,1},{3,2},{4,3},{5,4},{6,5},{7,6},{0,7},{9,8},{10,9},{11,1... | collective-permute-start | bytes 1277960 | tf_op jit(solution)/shard_map/ppermute | solution.py:13
  40.1 11.5 %collective-permute-start.1 = (f32[32,3328]{1,0:T(8,128)S(1)}, f32[32,3328]{1,0:T(8,128)S(1)}, u32[]{:S(2)}, u32[]{:S(2)}) collective-permute-start(f32[32,3328]{1,0:T(8,128)S(1)} %get-tuple-element.7), channel_id=1, source_target_pairs={{7,0},{0,1},{1,2},{2,3},{3,4},{4,5},{5,6},{6,7},{15,8},{8,9},{9,10... | collective-permute-start | bytes 1277960 | tf_op jit(solution)/shard_map/ppermute | solution.py:13
  42.1 9.6 %collective-permute-start.4 = (f32[32,3328]{1,0:T(8,128)S(1)}, f32[32,3328]{1,0:T(8,128)S(1)}, u32[]{:S(2)}, u32[]{:S(2)}) collective-permute-start(f32[32,3328]{1,0:T(8,128)S(1)} %get-tuple-element.8), channel_id=1, source_target_pairs={{1,0},{2,1},{3,2},{4,3},{5,4},{6,5},{7,6},{0,7},{9,8},{10,9},{11,1... | collective-permute-start | bytes 1277960 | tf_op jit(solution)/shard_map/ppermute | solution.py:13
  51.8 11.0 %collective-permute-start.2 = (f32[32,3328]{1,0:T(8,128)S(1)}, f32[32,3328]{1,0:T(8,128)S(1)}, u32[]{:S(2)}, u32[]{:S(2)}) collective-permute-start(f32[32,3328]{1,0:T(8,128)S(1)} %get-tuple-element.5), channel_id=1, source_target_pairs={{7,0},{0,1},{1,2},{2,3},{3,4},{4,5},{5,6},{6,7},{15,8},{8,9},{9,10... | collective-permute-start | bytes 1277960 | tf_op jit(solution)/shard_map/ppermute | solution.py:13
  54.2 9.6 %collective-permute-start.5 = (f32[32,3328]{1,0:T(8,128)S(1)}, f32[32,3328]{1,0:T(8,128)S(1)}, u32[]{:S(2)}, u32[]{:S(2)}) collective-permute-start(f32[32,3328]{1,0:T(8,128)S(1)} %get-tuple-element.6), channel_id=1, source_target_pairs={{1,0},{2,1},{3,2},{4,3},{5,4},{6,5},{7,6},{0,7},{9,8},{10,9},{11,1... | collective-permute-start | bytes 1277960 | tf_op jit(solution)/shard_map/ppermute | solution.py:13
where the time goes:
time: 87.8 us; the launch traced here: 87.4 us
  waiting for transfers between devices  24 us (27%)
  blocking collectives  21.9 us (25%)
  matrix products  16.3 us (19%)
  local copies, waits for them, and re-layouts  12.4 us (14%)
  starting transfers between devices  12.4 us (14%)
    ppermute x6, waiting for transfers between devices, shifted(): return lax.ppermute(block, axis, route)  24 us
    psum x1, blocking collectives, body(): density = lax.psum(partial_sum, 'band')  21.9 us
    ppermute x6, starting transfers between devices, shifted(): return lax.ppermute(block, axis, route)  12.4 us
    dot_general x1, matrix products, body(): jnp.einsum('ngb,gcb->gcn', grid_blocks, stacked, preferred_element_type=j...  9.38 us
    reshape x1, local copies, waits for them, and re-layouts, body(): slot_terms = slot_terms.reshape(block_count * capacity, row_len)  8.49 us
    dot_general x1, matrix products, body(): jnp.dot(selector, slot_terms, precision=lax.Precision.HIGHEST, preferred_...  6.29 us
    unnamed x6, local copies, waits for them, and re-layouts  2.86 us
  transfers between devices with their start and end apart: 6, of which 6 were waited for; matrix products, arithmetic and copies ran while one was open for 0% of the time, Pallas kernels for 0%

commit v1 on v0

--- a/solution.py
+++ b/solution.py
@@ -50,7 +50,13 @@
     owned = owned.reshape(ATOMS_DEV, proj_count, band_count)
     weighted = owned * occupations.reshape(1, 1, band_count)
     partial_sum = jnp.einsum("ain,ajn->aij", weighted, owned, precision=lax.Precision.HIGHEST)
-    density = lax.psum(partial_sum, "band")
+    count = lax.axis_size("band")
+    density, reach = (partial_sum, 1)
+    while reach < count:
+        density = density + lax.ppermute(
+            density, "band", [(i_2, i_2 ^ reach) for i_2 in range(count)]
+        )
+        reach = 2 * reach
     return density
 
 

time: 87.8 us -> 83 us (0.945)
  blocking collectives: 21.9 us -> 0 us
  waiting for transfers between devices: 24 us -> 37.1 us
  starting transfers between devices: 12.4 us -> 16.3 us
    psum x1 -> x0, blocking collectives: 21.9 us -> none  [body(): density = lax.psum(partial_sum, 'band')]
    ppermute x0 -> x2, waiting for transfers between devices: none -> 13.1 us  [body(): lax.ppermute(density, 'band', [(i_2, i_2 ^ reach) for i_2 in range(count)])]
    ppermute x0 -> x2, starting transfers between devices: none -> 3.91 us  [body(): lax.ppermute(density, 'band', [(i_2, i_2 ^ reach) for i_2 in range(count)])]
  transfers between devices with their start and end apart: 6 -> 8, of which waited for: 6 -> 8; matrix products, arithmetic and copies ran while one was open for 0% -> 0% of each run, Pallas kernels for 0% -> 0%
where the time goes in v1:
time: 83 us; the launch traced here: 82.6 us
  waiting for transfers between devices  37.1 us (45%)
  matrix products  16.3 us (20%)
  starting transfers between devices  16.3 us (20%)
  local copies, waits for them, and re-layouts  12.5 us (15%)
    ppermute x6, waiting for transfers between devices, shifted(): return lax.ppermute(block, axis, route)  24 us
    ppermute x2, waiting for transfers between devices, body(): lax.ppermute(density, 'band', [(i_2, i_2 ^ reach) for i_2 in range(count)])  13.1 us
    ppermute x6, starting transfers between devices, shifted(): return lax.ppermute(block, axis, route)  12.4 us
    dot_general x1, matrix products, body(): jnp.einsum('ngb,gcb->gcn', grid_blocks, stacked, preferred_element_type=j...  9.42 us
    reshape x1, local copies, waits for them, and re-layouts, body(): slot_terms = slot_terms.reshape(block_count * capacity, row_len)  8.49 us
    dot_general x1, matrix products, body(): jnp.dot(selector, slot_terms, precision=lax.Precision.HIGHEST, preferred_...  6.29 us
    ppermute x2, starting transfers between devices, body(): lax.ppermute(density, 'band', [(i_2, i_2 ^ reach) for i_2 in range(count)])  3.91 us
    unnamed x6, local copies, waits for them, and re-layouts  2.86 us
  transfers between devices with their start and end apart: 8, of which 8 were waited for; matrix products, arithmetic and copies ran while one was open for 0% of the time, Pallas kernels for 0%

profile of v1, /device:TPU:0, one launch (start us, length us, event | category | flops | bytes accessed | tf_op | source)
XLA Modules:
  0.0 82.6 jit_solution(6742691558252321003)
XLA Ops:
  0.0 2.8 %copy.8 = bf16[64,8,13,256]{3,0,2,1:T(8,128)(2,1)S(1)} copy(bf16[64,8,13,256]{3,1,2,0:T(8,128)(2,1)} %param.5) | data formatting | bytes 6815744 | tf_op args[1]
  2.8 9.4 %fusion = f32[64,104,256]{2,1,0:T(8,128)} fusion(bf16[32,64,8,256]{3,2,1,0:T(8,128)(2,1)} %bitcast.8, bf16[64,104,256]{2,0,1:T(8,128)(2,1)S(1)} %bitcast.7), kind=kOutput, calls=%fused_computation | convolution fusion | flops 872415232 | bytes 18612224 | tf_op jit(solution)/shard_map/ngb,gcb->gcn/dot_general | solution.py:25
  12.2 8.5 %reshape.103 = f32[512,3328]{1,0:T(8,128)} reshape(f32[64,104,256]{2,1,0:T(8,128)} %fusion) | data formatting | bytes 13631488 | tf_op jit(solution)/shard_map/reshape | solution.py:28
  20.8 0.1 reshape.100
  20.9 6.3 %fusion.6 = f32[224,3328]{1,0:T(8,128)S(1)} fusion(f32[512,3328]{1,0:T(8,128)} %reshape.103, s32[512]{0:T(512)S(1)} %fusion.15), kind=kOutput, calls=%fused_computation.7 | convolution fusion | flops 4580294656 | bytes 9799680 | tf_op jit(solution)/shard_map/dot_general | solution.py:38
  27.3 0.5 collective-permute-start
  27.8 4.1 %collective-permute-start.3 = (f32[32,3328]{1,0:T(8,128)S(1)}, f32[32,3328]{1,0:T(8,128)S(1)}, u32[]{:S(2)}, u32[]{:S(2)}) collective-permute-start(f32[32,3328]{1,0:T(8,128)S(1)} %get-tuple-element.10), channel_id=1, source_target_pairs={{1,0},{2,1},{3,2},{4,3},{5,4},{6,5},{7,6},{0,7},{9,8},{10,9},{11,1... | collective-permute-start | bytes 1277960 | tf_op jit(solution)/shard_map/ppermute | solution.py:13
  31.9 7.7 %collective-permute-done = f32[32,3328]{1,0:T(8,128)S(1)} collective-permute-done((f32[32,3328]{1,0:T(8,128)S(1)}, f32[32,3328]{1,0:T(8,128)S(1)}, u32[]{:S(2)}, u32[]{:S(2)}) %collective-permute-start) | collective-permute-done | bytes 426016 | tf_op jit(solution)/shard_map/ppermute | solution.py:13
  39.6 0.4 collective-permute-done.3
  40.1 2.0 %collective-permute-start.1 = (f32[32,3328]{1,0:T(8,128)S(1)}, f32[32,3328]{1,0:T(8,128)S(1)}, u32[]{:S(2)}, u32[]{:S(2)}) collective-permute-start(f32[32,3328]{1,0:T(8,128)S(1)} %get-tuple-element.7), channel_id=1, source_target_pairs={{7,0},{0,1},{1,2},{2,3},{3,4},{4,5},{5,6},{6,7},{15,8},{8,9},{9,10... | collective-permute-start | bytes 1277960 | tf_op jit(solution)/shard_map/ppermute | solution.py:13
  42.2 1.8 %collective-permute-start.4 = (f32[32,3328]{1,0:T(8,128)S(1)}, f32[32,3328]{1,0:T(8,128)S(1)}, u32[]{:S(2)}, u32[]{:S(2)}) collective-permute-start(f32[32,3328]{1,0:T(8,128)S(1)} %get-tuple-element.8), channel_id=1, source_target_pairs={{1,0},{2,1},{3,2},{4,3},{5,4},{6,5},{7,6},{0,7},{9,8},{10,9},{11,1... | collective-permute-start | bytes 1277960 | tf_op jit(solution)/shard_map/ppermute | solution.py:13
  44.0 7.6 %collective-permute-done.1 = f32[32,3328]{1,0:T(8,128)S(1)} collective-permute-done((f32[32,3328]{1,0:T(8,128)S(1)}, f32[32,3328]{1,0:T(8,128)S(1)}, u32[]{:S(2)}, u32[]{:S(2)}) %collective-permute-start.1) | collective-permute-done | bytes 426016 | tf_op jit(solution)/shard_map/ppermute | solution.py:13
  51.6 0.2 collective-permute-done.4
  51.8 2.5 %collective-permute-start.2 = (f32[32,3328]{1,0:T(8,128)S(1)}, f32[32,3328]{1,0:T(8,128)S(1)}, u32[]{:S(2)}, u32[]{:S(2)}) collective-permute-start(f32[32,3328]{1,0:T(8,128)S(1)} %get-tuple-element.5), channel_id=1, source_target_pairs={{7,0},{0,1},{1,2},{2,3},{3,4},{4,5},{5,6},{6,7},{15,8},{8,9},{9,10... | collective-permute-start | bytes 1277960 | tf_op jit(solution)/shard_map/ppermute | solution.py:13
  54.3 1.4 %collective-permute-start.5 = (f32[32,3328]{1,0:T(8,128)S(1)}, f32[32,3328]{1,0:T(8,128)S(1)}, u32[]{:S(2)}, u32[]{:S(2)}) collective-permute-start(f32[32,3328]{1,0:T(8,128)S(1)} %get-tuple-element.6), channel_id=1, source_target_pairs={{1,0},{2,1},{3,2},{4,3},{5,4},{6,5},{7,6},{0,7},{9,8},{10,9},{11,1... | collective-permute-start | bytes 1277960 | tf_op jit(solution)/shard_map/ppermute | solution.py:13
  55.7 7.1 %collective-permute-done.2 = f32[32,3328]{1,0:T(8,128)S(1)} collective-permute-done((f32[32,3328]{1,0:T(8,128)S(1)}, f32[32,3328]{1,0:T(8,128)S(1)}, u32[]{:S(2)}, u32[]{:S(2)}) %collective-permute-start.2) | collective-permute-done | bytes 426016 | tf_op jit(solution)/shard_map/ppermute | solution.py:13
  62.9 1.0 %collective-permute-done.5 = f32[32,3328]{1,0:T(8,128)S(1)} collective-permute-done((f32[32,3328]{1,0:T(8,128)S(1)}, f32[32,3328]{1,0:T(8,128)S(1)}, u32[]{:S(2)}, u32[]{:S(2)}) %collective-permute-start.5) | collective-permute-done | bytes 426016 | tf_op jit(solution)/shard_map/ppermute | solution.py:13
  63.9 0.1 reshape.104
  64.1 0.6 fusion.4
  64.7 1.9 %collective-permute-start.6 = (f32[32,13,13]{2,1,0:T(8,128)S(1)}, f32[32,13,13]{2,1,0:T(8,128)S(1)}, u32[]{:S(2)}, u32[]{:S(2)}) collective-permute-start(f32[32,13,13]{2,1,0:T(8,128)S(1)} %fusion.4), channel_id=1, source_target_pairs={{0,8},{8,0},{16,24},{24,16},{1,9},{9,1},{17,25},{25,17},{2,10},{10... | collective-permute-start | bytes 64904 | tf_op jit(solution)/shard_map/ppermute | solution.py:56
  66.6 6.1 %collective-permute-done.6 = f32[32,13,13]{2,1,0:T(8,128)S(1)} collective-permute-done((f32[32,13,13]{2,1,0:T(8,128)S(1)}, f32[32,13,13]{2,1,0:T(8,128)S(1)}, u32[]{:S(2)}, u32[]{:S(2)}) %collective-permute-start.6) | collective-permute-done | bytes 21664 | tf_op jit(solution)/shard_map/ppermute | solution.py:56
  72.7 2.0 %collective-permute-start.7 = (f32[32,13,13]{2,1,0:T(8,128)S(1)}, f32[32,13,13]{2,1,0:T(8,128)S(1)}, u32[]{:S(2)}, u32[]{:S(2)}) collective-permute-start(f32[32,13,13]{2,1,0:T(8,128)S(1)} %add.75), channel_id=1, source_target_pairs={{0,16},{8,24},{16,0},{24,8},{1,17},{9,25},{17,1},{25,9},{2,18},{10... | collective-permute-start | bytes 64904 | tf_op jit(solution)/shard_map/ppermute | solution.py:56
  74.7 7.0 %collective-permute-done.7 = f32[32,13,13]{2,1,0:T(8,128)S(1)} collective-permute-done((f32[32,13,13]{2,1,0:T(8,128)S(1)}, f32[32,13,13]{2,1,0:T(8,128)S(1)}, u32[]{:S(2)}, u32[]{:S(2)}) %collective-permute-start.7) | collective-permute-done | bytes 21664 | tf_op jit(solution)/shard_map/ppermute | solution.py:56
  81.8 0.8 copy.11
  (12 shorter events, 0.5 us)
Async XLA Ops:
  12.2 8.5 %copy-start = (s32[64,8]{0,1:T(8,128)S(1)}, s32[64,8]{0,1:T(8,128)}, u32[]{:S(2)}) copy-start(s32[64,8]{0,1:T(8,128)} %param.6) | copy-start | bytes 6148
  27.3 12.3 %collective-permute-start = (f32[32,3328]{1,0:T(8,128)S(1)}, f32[32,3328]{1,0:T(8,128)S(1)}, u32[]{:S(2)}, u32[]{:S(2)}) collective-permute-start(f32[32,3328]{1,0:T(8,128)S(1)} %get-tuple-element.9), channel_id=1, source_target_pairs={{7,0},{0,1},{1,2},{2,3},{3,4},{4,5},{5,6},{6,7},{15,8},{8,9},{9,10... | collective-permute-start | bytes 1277960 | tf_op jit(solution)/shard_map/ppermute | solution.py:13
  27.8 36.3 %copy-start.1 = (f32[256]{0:T(256)S(1)}, f32[256]{0:T(256)}, u32[]{:S(2)}) copy-start(f32[256]{0:T(256)} %param.7) | copy-start | bytes 3076
  27.8 12.2 %collective-permute-start.3 = (f32[32,3328]{1,0:T(8,128)S(1)}, f32[32,3328]{1,0:T(8,128)S(1)}, u32[]{:S(2)}, u32[]{:S(2)}) collective-permute-start(f32[32,3328]{1,0:T(8,128)S(1)} %get-tuple-element.10), channel_id=1, source_target_pairs={{1,0},{2,1},{3,2},{4,3},{5,4},{6,5},{7,6},{0,7},{9,8},{10,9},{11,1... | collective-permute-start | bytes 1277960 | tf_op jit(solution)/shard_map/ppermute | solution.py:13
  40.1 11.5 %collective-permute-start.1 = (f32[32,3328]{1,0:T(8,128)S(1)}, f32[32,3328]{1,0:T(8,128)S(1)}, u32[]{:S(2)}, u32[]{:S(2)}) collective-permute-start(f32[32,3328]{1,0:T(8,128)S(1)} %get-tuple-element.7), channel_id=1, source_target_pairs={{7,0},{0,1},{1,2},{2,3},{3,4},{4,5},{5,6},{6,7},{15,8},{8,9},{9,10... | collective-permute-start | bytes 1277960 | tf_op jit(solution)/shard_map/ppermute | solution.py:13
  42.2 9.6 %collective-permute-start.4 = (f32[32,3328]{1,0:T(8,128)S(1)}, f32[32,3328]{1,0:T(8,128)S(1)}, u32[]{:S(2)}, u32[]{:S(2)}) collective-permute-start(f32[32,3328]{1,0:T(8,128)S(1)} %get-tuple-element.8), channel_id=1, source_target_pairs={{1,0},{2,1},{3,2},{4,3},{5,4},{6,5},{7,6},{0,7},{9,8},{10,9},{11,1... | collective-permute-start | bytes 1277960 | tf_op jit(solution)/shard_map/ppermute | solution.py:13
  51.8 11.0 %collective-permute-start.2 = (f32[32,3328]{1,0:T(8,128)S(1)}, f32[32,3328]{1,0:T(8,128)S(1)}, u32[]{:S(2)}, u32[]{:S(2)}) collective-permute-start(f32[32,3328]{1,0:T(8,128)S(1)} %get-tuple-element.5), channel_id=1, source_target_pairs={{7,0},{0,1},{1,2},{2,3},{3,4},{4,5},{5,6},{6,7},{15,8},{8,9},{9,10... | collective-permute-start | bytes 1277960 | tf_op jit(solution)/shard_map/ppermute | solution.py:13
  54.3 9.6 %collective-permute-start.5 = (f32[32,3328]{1,0:T(8,128)S(1)}, f32[32,3328]{1,0:T(8,128)S(1)}, u32[]{:S(2)}, u32[]{:S(2)}) collective-permute-start(f32[32,3328]{1,0:T(8,128)S(1)} %get-tuple-element.6), channel_id=1, source_target_pairs={{1,0},{2,1},{3,2},{4,3},{5,4},{6,5},{7,6},{0,7},{9,8},{10,9},{11,1... | collective-permute-start | bytes 1277960 | tf_op jit(solution)/shard_map/ppermute | solution.py:13
  64.7 8.0 %collective-permute-start.6 = (f32[32,13,13]{2,1,0:T(8,128)S(1)}, f32[32,13,13]{2,1,0:T(8,128)S(1)}, u32[]{:S(2)}, u32[]{:S(2)}) collective-permute-start(f32[32,13,13]{2,1,0:T(8,128)S(1)} %fusion.4), channel_id=1, source_target_pairs={{0,8},{8,0},{16,24},{24,16},{1,9},{9,1},{17,25},{25,17},{2,10},{10... | collective-permute-start | bytes 64904 | tf_op jit(solution)/shard_map/ppermute | solution.py:56
  72.7 9.0 %collective-permute-start.7 = (f32[32,13,13]{2,1,0:T(8,128)S(1)}, f32[32,13,13]{2,1,0:T(8,128)S(1)}, u32[]{:S(2)}, u32[]{:S(2)}) collective-permute-start(f32[32,13,13]{2,1,0:T(8,128)S(1)} %add.75), channel_id=1, source_target_pairs={{0,16},{8,24},{16,0},{24,8},{1,17},{9,25},{17,1},{25,9},{2,18},{10... | collective-permute-start | bytes 64904 | tf_op jit(solution)/shard_map/ppermute | solution.py:56
